TPU v7x, 32 devices: a whole 2x2x4 slice. The times are simulated.
32 devices in a mesh: dp: 8 (over y, x, core), tensor: 4 (over z).
Axes of the slice: x: 2, y: 2, z: 4, core: 2. Of those that a mesh axis runs over, the one named last changes fastest.
Arguments:
- tokens: bfloat16 [256, 6144], P('dp', 'tensor'), may hold values from -6 to 6
- router_weight: bfloat16 [6144, 8], P('tensor'), may hold values from -0.078125 to 0.078125
- expert_ids: int32 [256, 2], P('dp'), may hold values from 0 to 7, all different within a row; in each aligned block of 32 rows (0 to 31, 32 to 63, ...) at most 12 rows name the same one
- w_gate: bfloat16 [8, 6144, 12288], P('dp', None, 'tensor'), may hold values from -0.078125 to 0.078125
- w_up: bfloat16 [8, 6144, 12288], P('dp', None, 'tensor'), may hold values from -0.078125 to 0.078125
- w_down: bfloat16 [8, 12288, 6144], P('dp', 'tensor'), may hold values from -0.0546875 to 0.0546875
Outputs:
- moe_out: bfloat16 [256, 6144], P('dp', 'tensor')
Inputs may be any that keep to these rules, and one draw needn't show every extreme that they name: `expert_ids`: the two experts of a token differ. In each aligned block of 32 rows (the rows of one index of dp) no expert is named by more than 12 rows, a bound that some blocks reach.
All inputs are finite; a program needn't handle non-finite values.
Results may differ from a plain program's by a relative error of at most 0.022.
Values may be sent and summed in bfloat16 or wider, within the bound.
A program may use at most 192 MiB of HBM per device.

v0:
```python
import functools

import jax
import jax.numpy as jnp
from jax import lax
from jax.experimental import pallas as pl
from jax.experimental.pallas import tpu as pltpu
from jax.sharding import PartitionSpec as P

EXPERTS = 8
CAP = 12
PAD = 16
LAG = 4
SLOTS = 16
F32 = jnp.float32
BF16 = jnp.bfloat16


def body(dp, nt, n, sub, pps, slots, tok_ref, rw_ref, ids_ref, wg_ref, wu_ref, wd_ref, out_ref,
         wbuf, rows, packed, hidden, ret_out, ret_in, ztok, zout, zin, own, lg_out, lg_in, hits, wmat,
         w_sem, zt_send, zt_recv, lg_send, lg_recv, d_send, d_recv, r_send, r_recv, zo_send, zo_recv):
    me = lax.axis_index("dp")
    t = lax.axis_index("tensor")
    toks, share = tok_ref.shape
    depth, ff = wg_ref.shape
    width = dp * PAD
    groups = dp // EXPERTS
    chunks = ff // n
    cb = pps * n
    steps = nt * sub
    units = 2 * chunks + steps
    mesh = pl.DeviceIdType.MESH

    def column(s):
        zi = s // sub
        half = nt // 2
        off = jnp.where(zi % 2 == 0, half - zi // 2, half + (zi + 1) // 2)
        q = lax.rem(t + off, nt)
        return q, s % sub

    def load(u, act):
        slot = lax.rem(u, slots)

        @pl.when(u < 2 * chunks)
        def _():
            cols = pl.ds(pl.multiple_of((u // 2) * n, n), n)

            @pl.when(u % 2 == 0)
            def _():
                act(pltpu.make_async_copy(wg_ref.at[:, cols], wbuf.at[slot], w_sem.at[slot]))

            @pl.when(u % 2 == 1)
            def _():
                act(pltpu.make_async_copy(wu_ref.at[:, cols], wbuf.at[slot], w_sem.at[slot]))

        @pl.when((u >= 2 * chunks) & (u < units))
        def _():
            q, j = column(u - 2 * chunks)
            for k in range(pps):
                cols = pl.ds(pl.multiple_of(q * share + j * cb + k * n, n), n)
                act(pltpu.make_async_copy(
                    wd_ref.at[:, cols], wbuf.at[slot, pl.ds(k * ff, ff)], w_sem2(slot, k)))

    def w_sem2(slot, k):
        return w_sem.at[k * slots + slot]

    @pl.loop(0, min(slots, units))
    def _(u):
        load(u, lambda c: c.start())

    rows[...] = jnp.zeros_like(rows)
    ret_in[...] = jnp.zeros_like(ret_in)
    barrier = pltpu.get_barrier_semaphore()

    @pl.loop(1, dp)
    def _(i):
        pl.semaphore_signal(barrier, inc=1, device_id={"dp": lax.rem(me + i, dp)}, device_id_type=mesh)

    @pl.loop(1, nt)
    def _(i):
        pl.semaphore_signal(barrier, inc=1, device_id={"tensor": lax.rem(t + i, nt)}, device_id_type=mesh)

    pl.semaphore_wait(barrier, dp + nt - 2)

    @pl.loop(1, nt)
    def _(i):
        pltpu.make_async_remote_copy(
            tok_ref, ztok.at[t], zt_send.at[i], zt_recv.at[t],
            device_id={"tensor": lax.rem(t + i, nt)}, device_id_type=mesh).start()

    ids = ids_ref[...]
    lane = lax.broadcasted_iota(jnp.int32, (toks, width), 1)
    expert = lane // (PAD * groups)
    rank = (lane % PAD).astype(F32)
    named = [ids[:, k:k + 1] == expert for k in range(2)]
    counts = (named[0] | named[1]).astype(F32).astype(BF16)
    lower = (lax.broadcasted_iota(jnp.int32, (toks, toks), 0)
             > lax.broadcasted_iota(jnp.int32, (toks, toks), 1)).astype(F32).astype(BF16)
    before = jnp.dot(lower, counts, preferred_element_type=F32)
    at_rank = before == rank
    for k in range(2):
        hits[k] = (named[k] & at_rank).astype(F32)
    placing = ((named[0] | named[1]) & at_rank).astype(F32)

    def dispatch(src, value):
        cols = pl.ds(pl.multiple_of(src * share, share), share)
        block = lax.dot_general(placing.astype(BF16), value, (((0,), (0,)), ((), ())),
                                preferred_element_type=F32).astype(BF16)
        packed[src] = block.reshape(dp, PAD, share)
        rows[me, :, cols] = packed[src, me]

        @pl.loop(1, dp)
        def _(i):
            p = lax.rem(me + i, dp)
            pltpu.make_async_remote_copy(
                packed.at[src, p, pl.ds(0, PAD)], rows.at[me, pl.ds(0, PAD), cols],
                d_send.at[src], d_recv.at[src],
                device_id={"dp": p}, device_id_type=mesh).start()

    dispatch(t, tok_ref[...])
    lg_out[...] = jnp.zeros_like(lg_out)
    lg_out[:, 0:EXPERTS] = jnp.dot(tok_ref[...], rw_ref[...], preferred_element_type=F32)
    lg_in[t] = lg_out[...]

    @pl.loop(1, nt)
    def _(i):
        pltpu.make_async_remote_copy(
            lg_out, lg_in.at[t], lg_send.at[i], lg_recv.at[t],
            device_id={"tensor": lax.rem(t + i, nt)}, device_id_type=mesh).start()

    @pl.loop(1, nt)
    def _(i):
        src = lax.rem(t + jnp.where(i % 2 == 1, nt - (i + 1) // 2, i // 2), nt)
        pltpu.make_async_copy(ztok.at[src], ztok.at[src], zt_recv.at[src]).wait()
        dispatch(src, ztok[src])

    @pl.loop(1, nt)
    def _(i):
        src = lax.rem(t + i, nt)
        pltpu.make_async_copy(lg_in.at[src], lg_in.at[src], lg_recv.at[src]).wait()

    logits = jnp.sum(lg_in[...], axis=0)
    lane8 = lax.broadcasted_iota(jnp.int32, logits.shape, 1)
    chosen = [jnp.sum(jnp.where(lane8 == ids[:, k:k + 1], logits, 0.0), axis=1, keepdims=True)
              for k in range(2)]
    first = jax.nn.sigmoid(chosen[0] - chosen[1])
    w = hits[0] * first + hits[1] * (1.0 - first)
    for k in range(3):
        part = w.astype(BF16)
        wmat[k] = part
        w = w - part.astype(F32)

    @pl.loop(0, nt)
    def _(src):
        cols = pl.ds(pl.multiple_of(src * share, share), share)
        view = rows.at[pl.ds(0, dp - 1), pl.ds(0, PAD), cols]
        pltpu.make_async_copy(view, view, d_recv.at[src]).wait()

    @pl.loop(0, chunks)
    def _(c):
        vals = []
        for k in range(2):
            u = 2 * c + k
            slot = lax.rem(u, slots)
            pltpu.make_async_copy(wbuf.at[slot], wbuf.at[slot], w_sem.at[slot]).wait()
            vals.append(jnp.dot(rows[...].reshape(width, depth), wbuf[slot], preferred_element_type=F32))
            load(u + slots, lambda d: d.start())
        gate, up = vals
        hidden[:, pl.ds(pl.multiple_of(c * n, n), n)] = (gate / (1.0 + jnp.exp(-gate)) * up).astype(BF16)

    @pl.loop(0, steps + LAG)
    def _(s):
        @pl.when(s < steps)
        def _():
            u = 2 * chunks + s
            slot = lax.rem(u, slots)
            load(u, lambda d: d.wait())
            for k in range(pps):
                term = jnp.dot(hidden[...], wbuf[slot, pl.ds(k * ff, ff)], preferred_element_type=F32)
                ret_out[s, :, :, pl.ds(k * n, n)] = term.astype(BF16).reshape(dp, PAD, n)
            load(u + slots, lambda d: d.start())
            ret_in[s, me] = ret_out[s, me]

            @pl.loop(1, dp)
            def _(i):
                p = lax.rem(me + i, dp)
                pltpu.make_async_remote_copy(
                    ret_out.at[s, p, pl.ds(0, PAD)], ret_in.at[s, me, pl.ds(0, PAD)],
                    r_send.at[s], r_recv.at[s],
                    device_id={"dp": p}, device_id_type=mesh).start()

        @pl.when(s >= LAG)
        def _():
            b = s - LAG
            q, j = column(b)
            view = ret_in.at[b, pl.ds(0, dp - 1), pl.ds(0, PAD)]
            pltpu.make_async_copy(view, view, r_recv.at[b]).wait()
            back = ret_in[b].reshape(width, cb)
            mixed = jnp.dot(wmat[0], back, preferred_element_type=F32)
            for k in range(1, 3):
                mixed += jnp.dot(wmat[k], back, preferred_element_type=F32)

            @pl.when(b < steps - sub)
            def _():
                zout[b] = mixed.astype(BF16)
                pltpu.make_async_remote_copy(
                    zout.at[b], zin.at[t, j], zo_send.at[b], zo_recv.at[t * sub + j],
                    device_id={"tensor": q}, device_id_type=mesh).start()

            @pl.when(b >= steps - sub)
            def _():
                own[j] = mixed

    @pl.loop(1, nt)
    def _(i):
        src = lax.rem(t + i, nt)

        @pl.loop(0, sub)
        def _(j):
            pltpu.make_async_copy(zin.at[src, j], zin.at[src, j], zo_recv.at[src * sub + j]).wait()
            own[j] += zin[src, j].astype(F32)

    for j in range(sub):
        out_ref[:, j * cb:(j + 1) * cb] = own[j].astype(BF16)

    @pl.loop(1, nt)
    def _(i):
        pltpu.make_async_copy(tok_ref, tok_ref, zt_send.at[i]).wait()
        pltpu.make_async_copy(lg_out, lg_out, lg_send.at[i]).wait()

    @pl.loop(0, nt)
    def _(src):
        view = packed.at[src, pl.ds(0, dp - 1), pl.ds(0, PAD)]
        pltpu.make_async_copy(view, view, d_send.at[src]).wait()

    @pl.loop(0, steps)
    def _(s):
        view = ret_out.at[s, pl.ds(0, dp - 1), pl.ds(0, PAD)]
        pltpu.make_async_copy(view, view, r_send.at[s]).wait()

    @pl.loop(0, steps - sub)
    def _(s):
        pltpu.make_async_copy(zout.at[s], zout.at[s], zo_send.at[s]).wait()


def per_device(dp, nt, tokens, router_weight, expert_ids, w_gate, w_up, w_down):
    toks, share = tokens.shape
    _, depth, ff = w_gate.shape
    n = min(256, ff)
    sub = 1
    while share // (sub * n) * ff > depth or share % (sub * n):
        sub += 1
    pps = share // (sub * n)
    cb = pps * n
    steps = nt * sub
    width = dp * PAD
    slots = SLOTS
    dma = pltpu.SemaphoreType.DMA
    vm = pl.BlockSpec(memory_space=pltpu.VMEM)
    hbm = pl.BlockSpec(memory_space=pltpu.HBM)
    return pl.pallas_call(
        functools.partial(body, dp, nt, n, sub, pps, slots),
        out_shape=jax.ShapeDtypeStruct((toks, share), BF16),
        in_specs=[vm, vm, vm, hbm, hbm, hbm],
        out_specs=vm,
        scratch_shapes=[
            pltpu.VMEM((slots, depth, n), BF16),
            pltpu.VMEM((dp, PAD, depth), BF16),
            pltpu.VMEM((nt, dp, PAD, share), BF16),
            pltpu.VMEM((width, ff), BF16),
            pltpu.VMEM((steps, dp, PAD, cb), BF16),
            pltpu.VMEM((steps, dp, PAD, cb), BF16),
            pltpu.VMEM((nt, toks, share), BF16),
            pltpu.VMEM((steps, toks, cb), BF16),
            pltpu.VMEM((nt, sub, toks, cb), BF16),
            pltpu.VMEM((sub, toks, cb), F32),
            pltpu.VMEM((toks, 128), F32),
            pltpu.VMEM((nt, toks, 128), F32),
            pltpu.VMEM((2, toks, width), F32),
            pltpu.VMEM((3, toks, width), BF16),
            dma((slots * pps,)),
            dma((nt,)), dma((nt,)), dma((nt,)), dma((nt,)),
            dma((nt,)), dma((nt,)), dma((steps,)), dma((steps,)),
            dma((steps,)), dma((steps,)),
        ],
        compiler_params=pltpu.CompilerParams(
            collective_id=0, has_side_effects=True, vmem_limit_bytes=67043328),
    )(tokens, router_weight, expert_ids, w_gate[0], w_up[0], w_down[0])


def solution(mesh):
    return jax.shard_map(
        functools.partial(per_device, mesh.shape["dp"], mesh.shape["tensor"]),
        mesh=mesh,
        in_specs=(
            P("dp", "tensor"),
            P("tensor", None),
            P("dp", None),
            P("dp", None, "tensor"),
            P("dp", None, "tensor"),
            P("dp", "tensor", None),
        ),
        out_specs=P("dp", "tensor"),
        check_vma=False,
    )
```

profile of v0, /device:TPU:0, one launch (start us, length us, event | category | flops | bytes accessed | tf_op | source)
XLA Modules:
  0.0 75.3 jit_solution(5413551305177722543)
XLA Ops:
  0.0 1.4 %copy.8.ids_ref = s32[32,2]{1,0:T(8,128)} copy(s32[32,2]{0,1:T(2,128)} %param.8) | data formatting | bytes 512 | tf_op args[2]
  1.4 1.6 %copy.7.rw_ref = bf16[1536,8]{1,0:T(8,128)(2,1)} copy(bf16[1536,8]{0,1:T(8,128)(2,1)} %param.7) | data formatting | bytes 49152 | tf_op args[1]
  3.0 70.7 %shard_map.64 = bf16[32,1536]{1,0:T(8,128)(2,1)} custom-call(bf16[32,1536]{1,0:T(8,128)(2,1)} %tok_ref.1, bf16[1536,8]{1,0:T(8,128)(2,1)} %copy.7.rw_ref, s32[32,2]{1,0:T(8,128)} %copy.8.ids_ref, bf16[6144,3072]{1,0:T(8,128)(2,1)} %bitcast.3, bf16[6144,3072]{1,0:T(8,128)(2,1)} %bitcast.4, bf16[3072,6144]{1,0:T(8,128)(2,1)} %bitcast.5), custom_call_target="tpu_custom_call" | custom-call | tf_op jit(solution)/shard_map/pallas_call | solution.py:261
  73.8 1.5 %copy.10 = bf16[32,1536]{1,0:T(8,128)(2,1)} copy(bf16[32,1536]{1,0:T(8,128)(2,1)} %shard_map.64) | data formatting | bytes 196608
where the time goes:
time: 75.5 us; the launch traced here: 75.3 us
  Pallas kernels  70.7 us (94%)
  local copies, waits for them, and re-layouts  4.55 us (6%)
    pallas_call x1, Pallas kernels, per_device(): pl.pallas_call(functools.partial(body, dp, nt, n, sub, pps, slots), out_s...  70.7 us
    unnamed x3, local copies, waits for them, and re-layouts  4.55 us

commit v1 on v0

v1 whole, which is shorter than its diff:
```python
import functools

import jax
import jax.numpy as jnp
from jax import lax
from jax.experimental import pallas as pl
from jax.experimental.pallas import tpu as pltpu
from jax.sharding import PartitionSpec as P

EXPERTS = 8
PAD = 16
PIECES = ((0, 8), (8, 4))
LAG = 5
SLOTS = 15
FIRST = 2
AHEAD = 3
LANES = 128
F32 = jnp.float32
BF16 = jnp.bfloat16


def body(dp, nt, n, cb, slots, tok_hbm, rw_hbm, ids_hbm, wg_ref, wu_ref, wd_ref, out_ref,
         wbuf, rows, packed, acc, hidden, ret_out, ret_in, ztok, zout, zin, own, lg_out, lg_in,
         hits, wmat, tokv, rwv, idsv,
         in_sem, w_sem, zt_send, zt_recv, lg_send, lg_recv, d_send, d_recv, r_send, r_recv,
         zo_send, zo_recv):
    me = lax.axis_index("dp")
    t = lax.axis_index("tensor")
    toks, share = tokv.shape
    _, ff = wg_ref.shape
    width = dp * PAD
    groups = dp // EXPERTS
    chunks = ff // n
    kb = min(ff, share)
    kbs = ff // kb
    sub = share // (2 * cb)
    steps = nt * sub
    first_units = nt * chunks
    units = first_units + steps
    mesh = pl.DeviceIdType.MESH

    def order(i):
        near = jnp.where(i % 2 == 1, t - (i + 1) // 2, t + (i + 1) // 2)
        far = jnp.where(t < nt - 1 - t, i, nt - 1 - i)
        return jnp.where(i <= 2 * jnp.minimum(t, nt - 1 - t), near, far)

    def column(s):
        return order(nt - 1 - s // sub), s % sub

    def load(u, act):
        slot = lax.rem(u, slots)

        @pl.when(u < first_units)
        def _():
            deep = pl.ds(pl.multiple_of(order(u // chunks) * share, share), share)
            cols = pl.ds(pl.multiple_of(lax.rem(u, chunks) * n, n), n)
            act(pltpu.make_async_copy(wg_ref.at[deep, cols], wbuf.at[slot, 0], w_sem.at[slot]))
            act(pltpu.make_async_copy(wu_ref.at[deep, cols], wbuf.at[slot, 1], w_sem.at[slots + slot]))

        @pl.when((u >= first_units) & (u < units))
        def _():
            q, j = column(u - first_units)
            for h in range(2):
                for b in range(kbs):
                    cols = pl.ds(pl.multiple_of(q * share + (2 * j + h) * cb, cb), cb)
                    act(pltpu.make_async_copy(
                        wd_ref.at[pl.ds(b * kb, kb), cols],
                        wbuf.at[slot, h, pl.ds(0, kb), pl.ds(b * cb, cb)],
                        w_sem.at[(b * 2 + h) * slots + slot]))

    small = [pltpu.make_async_copy(a, b, in_sem.at[k]) for k, (a, b) in enumerate(
        ((tok_hbm, tokv), (ids_hbm, idsv), (rw_hbm, rwv)))]
    for c in small:
        c.start()

    @pl.loop(0, min(FIRST, units))
    def _(u):
        load(u, lambda c: c.start())

    rows[:, :, 8:PAD, :] = jnp.zeros((nt, dp, PAD - 8, share), BF16)
    ret_in[:, :, 8:PAD, :] = jnp.zeros((steps, dp, PAD - 8, 2 * cb), BF16)
    barrier = pltpu.get_barrier_semaphore()

    @pl.loop(1, dp)
    def _(i):
        pl.semaphore_signal(barrier, inc=1, device_id={"dp": lax.rem(me + i, dp)}, device_id_type=mesh)

    @pl.loop(1, nt)
    def _(i):
        pl.semaphore_signal(barrier, inc=1, device_id={"tensor": lax.rem(t + i, nt)}, device_id_type=mesh)

    @pl.loop(min(FIRST, units), min(slots, units))
    def _(u):
        load(u, lambda c: c.start())

    small[1].wait()
    ids = idsv[...]
    line = lax.broadcasted_iota(jnp.int32, (width, toks), 0)
    expert = line // (PAD * groups)
    rank = (line % PAD).astype(F32)
    named = [ids[k:k + 1, :] == expert for k in range(2)]
    counts = (named[0] | named[1]).astype(F32).astype(BF16)
    upper = (lax.broadcasted_iota(jnp.int32, (toks, toks), 0)
             < lax.broadcasted_iota(jnp.int32, (toks, toks), 1)).astype(F32).astype(BF16)
    before = jnp.dot(counts, upper, preferred_element_type=F32)
    at_rank = before == rank
    for k in range(2):
        hits[k] = (named[k] & at_rank).astype(F32)
    placing = ((named[0] | named[1]) & at_rank).astype(F32).astype(BF16)
    small[0].wait()
    small[2].wait()

    pl.semaphore_wait(barrier, dp + nt - 2)

    @pl.loop(1, nt)
    def _(i):
        pltpu.make_async_remote_copy(
            tokv, ztok.at[t], zt_send.at[i], zt_recv.at[t],
            device_id={"tensor": order(i)}, device_id_type=mesh).start()

    def dispatch(src, value):
        block = jnp.dot(placing, value, preferred_element_type=F32).astype(BF16)
        packed[src] = block.reshape(dp, PAD, share)
        rows[src, me] = packed[src, me]

        @pl.loop(1, dp)
        def _(i):
            p = lax.rem(me + i, dp)
            for k, (a, b) in enumerate(PIECES):
                pltpu.make_async_remote_copy(
                    packed.at[src, p, pl.ds(a, b)], rows.at[src, me, pl.ds(a, b)],
                    d_send.at[src, k], d_recv.at[src, k],
                    device_id={"dp": p}, device_id_type=mesh).start()

    def relay(i):
        src = order(i)
        pltpu.make_async_copy(ztok.at[src], ztok.at[src], zt_recv.at[src]).wait()
        dispatch(src, ztok[src])

    dispatch(t, tokv[...])
    lg_out[...] = jnp.zeros_like(lg_out)
    lg_out[:, 0:toks] = lax.dot_general(rwv[...], tokv[...], (((1,), (1,)), ((), ())),
                                        preferred_element_type=F32)
    lg_in[t] = lg_out[...]

    @pl.loop(1, nt)
    def _(i):
        pltpu.make_async_remote_copy(
            lg_out, lg_in.at[t], lg_send.at[i], lg_recv.at[t],
            device_id={"tensor": order(i)}, device_id_type=mesh).start()

    acc[...] = jnp.zeros_like(acc)

    @pl.loop(1, min(AHEAD, nt))
    def _(i):
        relay(i)

    def products(i, c):
        u = i * chunks + c
        slot = lax.rem(u, slots)
        for k in range(2):
            pltpu.make_async_copy(wbuf.at[slot, k], wbuf.at[slot, k], w_sem.at[k * slots + slot]).wait()
        src = order(i)
        lhs = rows[src].reshape(width, share)
        cols = pl.ds(pl.multiple_of(c * n, n), n)
        out = [acc[k, :, cols] + jnp.dot(lhs, wbuf[slot, k], preferred_element_type=F32)
               for k in range(2)]
        return u, cols, out

    def arrived(i):
        src = order(i)
        for k, (a, b) in enumerate(PIECES):
            view = rows.at[src, pl.ds(0, dp - 1), pl.ds(a, b)]
            pltpu.make_async_copy(view, view, d_recv.at[src, k]).wait()

    @pl.loop(0, nt - 1)
    def _(i):
        arrived(i)

        @pl.loop(0, chunks)
        def _(c):
            u, cols, out = products(i, c)
            for k in range(2):
                acc[k, :, cols] = out[k]
            load(u + slots, lambda d: d.start())

        @pl.when(i + AHEAD < nt)
        def _():
            relay(i + AHEAD)

    arrived(nt - 1)

    @pl.loop(0, chunks)
    def _(c):
        u, cols, (gate, up) = products(nt - 1, c)
        hidden[:, cols] = (gate / (1.0 + jnp.exp(-gate)) * up).astype(BF16)
        load(u + slots, lambda d: d.start())

    @pl.loop(1, nt)
    def _(i):
        src = order(i)
        pltpu.make_async_copy(lg_in.at[src], lg_in.at[src], lg_recv.at[src]).wait()

    logits = jnp.sum(lg_in[...], axis=0)[:, 0:toks]
    which = lax.broadcasted_iota(jnp.int32, logits.shape, 0)
    chosen = [jnp.sum(jnp.where(which == idsv[k:k + 1, :], logits, 0.0), axis=0, keepdims=True)
              for k in range(2)]
    first = jax.nn.sigmoid(chosen[0] - chosen[1])
    w = hits[0] * first + hits[1] * (1.0 - first)
    eye = (lax.broadcasted_iota(jnp.int32, (toks, toks), 0)
           == lax.broadcasted_iota(jnp.int32, (toks, toks), 1)).astype(F32).astype(BF16)
    for k in range(3):
        part = w.astype(BF16)
        wmat[k] = lax.dot_general(eye, part, (((1,), (1,)), ((), ())),
                                  preferred_element_type=F32).astype(BF16)
        w = w - part.astype(F32)

    @pl.loop(0, steps + LAG)
    def _(s):
        @pl.when(s < steps)
        def _():
            u = first_units + s
            slot = lax.rem(u, slots)
            load(u, lambda d: d.wait())
            for h in range(2):
                term = sum(jnp.dot(hidden[:, b * kb:(b + 1) * kb],
                                   wbuf[slot, h, 0:kb, b * cb:(b + 1) * cb],
                                   preferred_element_type=F32) for b in range(kbs))
                ret_out[s, :, :, pl.ds(h * cb, cb)] = term.astype(BF16).reshape(dp, PAD, cb)
            load(u + slots, lambda d: d.start())
            ret_in[s, me] = ret_out[s, me]

            @pl.loop(1, dp)
            def _(i):
                p = lax.rem(me + i, dp)
                for k, (a, b) in enumerate(PIECES):
                    pltpu.make_async_remote_copy(
                        ret_out.at[s, p, pl.ds(a, b)], ret_in.at[s, me, pl.ds(a, b)],
                        r_send.at[s, k], r_recv.at[s, k],
                        device_id={"dp": p}, device_id_type=mesh).start()

        @pl.when(s >= LAG)
        def _():
            b = s - LAG
            q, j = column(b)
            for k, (a, d) in enumerate(PIECES):
                view = ret_in.at[b, pl.ds(0, dp - 1), pl.ds(a, d)]
                pltpu.make_async_copy(view, view, r_recv.at[b, k]).wait()
            back = ret_in[b].reshape(width, 2 * cb)
            mixed = jnp.dot(wmat[0], back, preferred_element_type=F32)
            for k in range(1, 3):
                mixed += jnp.dot(wmat[k], back, preferred_element_type=F32)

            @pl.when(b < steps - sub)
            def _():
                zout[b] = mixed.astype(BF16)
                pltpu.make_async_remote_copy(
                    zout.at[b], zin.at[t, j], zo_send.at[b], zo_recv.at[t * sub + j],
                    device_id={"tensor": q}, device_id_type=mesh).start()

            @pl.when(b >= steps - sub)
            def _():
                own[j] = mixed

    @pl.loop(1, nt)
    def _(i):
        src = lax.rem(t + i, nt)

        @pl.loop(0, sub)
        def _(j):
            pltpu.make_async_copy(zin.at[src, j], zin.at[src, j], zo_recv.at[src * sub + j]).wait()
            own[j] += zin[src, j].astype(F32)

    for j in range(sub):
        out_ref[:, j * 2 * cb:(j + 1) * 2 * cb] = own[j].astype(BF16)

    @pl.loop(1, nt)
    def _(i):
        pltpu.make_async_copy(tokv, tokv, zt_send.at[i]).wait()
        pltpu.make_async_copy(lg_out, lg_out, lg_send.at[i]).wait()

    @pl.loop(0, nt)
    def _(src):
        for k, (a, d) in enumerate(PIECES):
            view = packed.at[src, pl.ds(0, dp - 1), pl.ds(a, d)]
            pltpu.make_async_copy(view, view, d_send.at[src, k]).wait()

    @pl.loop(0, steps)
    def _(s):
        for k, (a, d) in enumerate(PIECES):
            view = ret_out.at[s, pl.ds(0, dp - 1), pl.ds(a, d)]
            pltpu.make_async_copy(view, view, r_send.at[s, k]).wait()

    @pl.loop(0, steps - sub)
    def _(s):
        pltpu.make_async_copy(zout.at[s], zout.at[s], zo_send.at[s]).wait()


def per_device(dp, nt, tokens, router_weight, expert_ids, w_gate, w_up, w_down):
    toks, share = tokens.shape
    _, depth, ff = w_gate.shape
    n = min(512, ff)
    cb = n // (ff // min(ff, share))
    sub = share // (2 * cb)
    steps = nt * sub
    width = dp * PAD
    lanes = -(-toks // LANES) * LANES
    slots = SLOTS
    dma = pltpu.SemaphoreType.DMA
    vm = pl.BlockSpec(memory_space=pltpu.VMEM)
    hbm = pl.BlockSpec(memory_space=pltpu.HBM)
    return pl.pallas_call(
        functools.partial(body, dp, nt, n, cb, slots),
        out_shape=jax.ShapeDtypeStruct((toks, share), BF16),
        in_specs=[hbm] * 6,
        out_specs=vm,
        scratch_shapes=[
            pltpu.VMEM((slots, 2, share, n), BF16),
            pltpu.VMEM((nt, dp, PAD, share), BF16),
            pltpu.VMEM((nt, dp, PAD, share), BF16),
            pltpu.VMEM((2, width, ff), F32),
            pltpu.VMEM((width, ff), BF16),
            pltpu.VMEM((steps, dp, PAD, 2 * cb), BF16),
            pltpu.VMEM((steps, dp, PAD, 2 * cb), BF16),
            pltpu.VMEM((nt, toks, share), BF16),
            pltpu.VMEM((steps, toks, 2 * cb), BF16),
            pltpu.VMEM((nt, sub, toks, 2 * cb), BF16),
            pltpu.VMEM((sub, toks, 2 * cb), F32),
            pltpu.VMEM((EXPERTS, lanes), F32),
            pltpu.VMEM((nt, EXPERTS, lanes), F32),
            pltpu.VMEM((2, width, toks), F32),
            pltpu.VMEM((3, toks, width), BF16),
            pltpu.VMEM((toks, share), BF16),
            pltpu.VMEM((EXPERTS, share), BF16),
            pltpu.VMEM((2, toks), jnp.int32),
            dma((3,)),
            dma((2 * (ff // min(ff, share)) * slots,)),
            dma((nt,)), dma((nt,)), dma((nt,)), dma((nt,)),
            dma((nt, 2)), dma((nt, 2)), dma((steps, 2)), dma((steps, 2)),
            dma((steps,)), dma((steps,)),
        ],
        compiler_params=pltpu.CompilerParams(
            collective_id=0, has_side_effects=True, vmem_limit_bytes=67043328),
    )(tokens, router_weight.T, expert_ids.T, w_gate[0], w_up[0], w_down[0])


def solution(mesh):
    return jax.shard_map(
        functools.partial(per_device, mesh.shape["dp"], mesh.shape["tensor"]),
        mesh=mesh,
        in_specs=(
            P("dp", "tensor"),
            P("tensor", None),
            P("dp", None),
            P("dp", None, "tensor"),
            P("dp", None, "tensor"),
            P("dp", "tensor", None),
        ),
        out_specs=P("dp", "tensor"),
        check_vma=False,
    )
```

time: 75.5 us -> 50.1 us (0.66)
  Pallas kernels: 70.7 us -> 48.5 us
  local copies, waits for them, and re-layouts: 4.55 us -> 1.54 us
    pallas_call x1, Pallas kernels: 70.7 us -> 48.5 us  [per_device(): pl.pallas_call(functools.partial(body, dp, nt, n, cb, slots), out_shape=j...]
    unnamed x3 -> x1, local copies, waits for them, and re-layouts: 4.55 us -> 1.54 us
where the time goes in v1:
time: 50.1 us; the launch traced here: 50 us
  Pallas kernels  48.5 us (97%)
  local copies, waits for them, and re-layouts  1.54 us (3%)
    pallas_call x1, Pallas kernels, per_device(): pl.pallas_call(functools.partial(body, dp, nt, n, cb, slots), out_shape=j...  48.5 us
    unnamed x1, local copies, waits for them, and re-layouts  1.54 us

profile of v1, /device:TPU:0, one launch (start us, length us, event | category | flops | bytes accessed | tf_op | source)
XLA Modules:
  0.0 50.0 jit_solution(5650432738304165009)
XLA Ops:
  0.0 48.5 %shard_map.64 = bf16[32,1536]{1,0:T(8,128)(2,1)} custom-call(bf16[32,1536]{1,0:T(8,128)(2,1)} %tok_hbm.1, bf16[8,1536]{1,0:T(8,128)(2,1)} %bitcast.8, s32[2,32]{1,0:T(2,128)} %bitcast.9, bf16[6144,3072]{1,0:T(8,128)(2,1)} %bitcast.5, bf16[6144,3072]{1,0:T(8,128)(2,1)} %bitcast.6, bf16[3072,6144]{1,0:T(8,128)(2,1)} %bitcast.7), custom_call_target="tpu_custom_call" | custom-call | tf_op jit(solution)/shard_map/pallas_call | solution.py:312
  48.5 1.5 %copy.8 = bf16[32,1536]{1,0:T(8,128)(2,1)} copy(bf16[32,1536]{1,0:T(8,128)(2,1)} %shard_map.64) | data formatting | bytes 196608

commit v2 on v1

--- a/solution.py
+++ b/solution.py
@@ -10,19 +10,20 @@
 EXPERTS = 8
 PAD = 16
 PIECES = ((0, 8), (8, 4))
-LAG = 5
-SLOTS = 15
+LAG = 4
+SLOTS = 14
 FIRST = 2
 AHEAD = 3
+UNROLL = 2
 LANES = 128
 F32 = jnp.float32
 BF16 = jnp.bfloat16
 
 
 def body(dp, nt, n, cb, slots, tok_hbm, rw_hbm, ids_hbm, wg_ref, wu_ref, wd_ref, out_ref,
-         wbuf, rows, packed, acc, hidden, ret_out, ret_in, ztok, zout, zin, own, lg_out, lg_in,
+         wbuf, rows, packed, acc, hidden, ret_in, ztok, zout, zin, own, lg_out, lg_in,
          hits, wmat, tokv, rwv, idsv,
-         in_sem, w_sem, zt_send, zt_recv, lg_send, lg_recv, d_send, d_recv, r_send, r_recv,
+         in_sem, w_sem, own_send, zt_send, zt_recv, lg_send, lg_recv, d_send, d_recv, r_send, r_recv,
          zo_send, zo_recv):
     me = lax.axis_index("dp")
     t = lax.axis_index("tensor")
@@ -37,12 +38,17 @@
     steps = nt * sub
     first_units = nt * chunks
     units = first_units + steps
+    unroll = max(k for k in range(1, UNROLL + 1) if chunks % k == 0)
     mesh = pl.DeviceIdType.MESH
 
     def order(i):
         near = jnp.where(i % 2 == 1, t - (i + 1) // 2, t + (i + 1) // 2)
         far = jnp.where(t < nt - 1 - t, i, nt - 1 - i)
         return jnp.where(i <= 2 * jnp.minimum(t, nt - 1 - t), near, far)
+
+    sides = ((t > 0, jnp.maximum(t - 1, 0)), (t < nt - 1, jnp.minimum(t + 1, nt - 1)))
+    inner = (t > 0) & (t < nt - 1)
+    half = toks // 2
 
     def column(s):
         return order(nt - 1 - s // sub), s % sub
@@ -85,9 +91,10 @@
     def _(i):
         pl.semaphore_signal(barrier, inc=1, device_id={"dp": lax.rem(me + i, dp)}, device_id_type=mesh)
 
-    @pl.loop(1, nt)
-    def _(i):
-        pl.semaphore_signal(barrier, inc=1, device_id={"tensor": lax.rem(t + i, nt)}, device_id_type=mesh)
+    for there, beside in sides:
+        @pl.when(there)
+        def _():
+            pl.semaphore_signal(barrier, inc=1, device_id={"tensor": beside}, device_id_type=mesh)
 
     @pl.loop(min(FIRST, units), min(slots, units))
     def _(u):
@@ -110,13 +117,18 @@
     small[0].wait()
     small[2].wait()
 
-    pl.semaphore_wait(barrier, dp + nt - 2)
-
-    @pl.loop(1, nt)
-    def _(i):
-        pltpu.make_async_remote_copy(
-            tokv, ztok.at[t], zt_send.at[i], zt_recv.at[t],
-            device_id={"tensor": order(i)}, device_id_type=mesh).start()
+    pl.semaphore_wait(barrier, dp - 1 + jnp.where(t > 0, 1, 0) + jnp.where(t < nt - 1, 1, 0))
+
+    def piece(ref, h):
+        return ref.at[pl.ds(h * half, half)]
+
+    for h in range(2):
+        for k, (there, beside) in enumerate(sides):
+            @pl.when(there)
+            def _():
+                pltpu.make_async_remote_copy(
+                    piece(tokv, h), piece(ztok.at[t], h), own_send.at[2 * h + k], zt_recv.at[t, h],
+                    device_id={"tensor": beside}, device_id_type=mesh).start()
 
     def dispatch(src, value):
         block = jnp.dot(placing, value, preferred_element_type=F32).astype(BF16)
@@ -132,9 +144,21 @@
                     d_send.at[src, k], d_recv.at[src, k],
                     device_id={"dp": p}, device_id_type=mesh).start()
 
+    def forward(i):
+        src = order(i)
+        for h in range(2):
+            block = piece(ztok.at[src], h)
+            pltpu.make_async_copy(block, block, zt_recv.at[src, h]).wait()
+            for k, (there, beside) in enumerate(sides):
+                @pl.when(there & ((src > t) if k == 0 else (src < t)))
+                def _():
+                    pltpu.make_async_remote_copy(
+                        block, block, zt_send.at[src, h], zt_recv.at[src, h],
+                        device_id={"tensor": beside}, device_id_type=mesh).start()
+
     def relay(i):
+        forward(i)
         src = order(i)
-        pltpu.make_async_copy(ztok.at[src], ztok.at[src], zt_recv.at[src]).wait()
         dispatch(src, ztok[src])
 
     dispatch(t, tokv[...])
@@ -143,29 +167,39 @@
                                         preferred_element_type=F32)
     lg_in[t] = lg_out[...]
 
-    @pl.loop(1, nt)
-    def _(i):
-        pltpu.make_async_remote_copy(
-            lg_out, lg_in.at[t], lg_send.at[i], lg_recv.at[t],
-            device_id={"tensor": order(i)}, device_id_type=mesh).start()
-
     acc[...] = jnp.zeros_like(acc)
 
-    @pl.loop(1, min(AHEAD, nt))
-    def _(i):
-        relay(i)
-
-    def products(i, c):
-        u = i * chunks + c
-        slot = lax.rem(u, slots)
+    ahead = jnp.where(inner, AHEAD + 1, AHEAD)
+
+    @pl.loop(1, min(AHEAD + 1, nt))
+    def _(i):
+        @pl.when(i < ahead)
+        def _():
+            relay(i)
+
+    def products(i, g, finish):
+        src = order(i)
+        first = i * chunks + g * unroll
+        slot = [lax.rem(first + j, slots) for j in range(unroll)]
+        for j in range(unroll):
+            for k in range(2):
+                pltpu.make_async_copy(wbuf.at[slot[j], k], wbuf.at[slot[j], k],
+                                      w_sem.at[k * slots + slot[j]]).wait()
+        lhs = rows[src].reshape(width, share)
+        for j in range(unroll):
+            cols = pl.ds(pl.multiple_of((g * unroll + j) * n, n), n)
+            finish(cols, [acc[k, :, cols] + jnp.dot(lhs, wbuf[slot[j], k], preferred_element_type=F32)
+                          for k in range(2)])
+        for j in range(unroll):
+            load(first + j + slots, lambda d: d.start())
+
+    def keep(cols, out):
         for k in range(2):
-            pltpu.make_async_copy(wbuf.at[slot, k], wbuf.at[slot, k], w_sem.at[k * slots + slot]).wait()
-        src = order(i)
-        lhs = rows[src].reshape(width, share)
-        cols = pl.ds(pl.multiple_of(c * n, n), n)
-        out = [acc[k, :, cols] + jnp.dot(lhs, wbuf[slot, k], preferred_element_type=F32)
-               for k in range(2)]
-        return u, cols, out
+            acc[k, :, cols] = out[k]
+
+    def activate(cols, out):
+        gate, up = out
+        hidden[:, cols] = (gate / (1.0 + jnp.exp(-gate)) * up).astype(BF16)
 
     def arrived(i):
         src = order(i)
@@ -177,43 +211,51 @@
     def _(i):
         arrived(i)
 
-        @pl.loop(0, chunks)
-        def _(c):
-            u, cols, out = products(i, c)
-            for k in range(2):
-                acc[k, :, cols] = out[k]
-            load(u + slots, lambda d: d.start())
-
-        @pl.when(i + AHEAD < nt)
-        def _():
-            relay(i + AHEAD)
+        @pl.loop(0, chunks // unroll)
+        def _(g):
+            products(i, g, keep)
+
+        @pl.when(i + ahead < nt)
+        def _():
+            relay(i + ahead)
+
+    @pl.loop(1, nt)
+    def _(i):
+        pltpu.make_async_remote_copy(
+            lg_out, lg_in.at[t], lg_send.at[i], lg_recv.at[t],
+            device_id={"tensor": order(i)}, device_id_type=mesh).start()
 
     arrived(nt - 1)
 
-    @pl.loop(0, chunks)
-    def _(c):
-        u, cols, (gate, up) = products(nt - 1, c)
-        hidden[:, cols] = (gate / (1.0 + jnp.exp(-gate)) * up).astype(BF16)
-        load(u + slots, lambda d: d.start())
-
-    @pl.loop(1, nt)
-    def _(i):
-        src = order(i)
-        pltpu.make_async_copy(lg_in.at[src], lg_in.at[src], lg_recv.at[src]).wait()
-
-    logits = jnp.sum(lg_in[...], axis=0)[:, 0:toks]
-    which = lax.broadcasted_iota(jnp.int32, logits.shape, 0)
-    chosen = [jnp.sum(jnp.where(which == idsv[k:k + 1, :], logits, 0.0), axis=0, keepdims=True)
-              for k in range(2)]
-    first = jax.nn.sigmoid(chosen[0] - chosen[1])
-    w = hits[0] * first + hits[1] * (1.0 - first)
-    eye = (lax.broadcasted_iota(jnp.int32, (toks, toks), 0)
-           == lax.broadcasted_iota(jnp.int32, (toks, toks), 1)).astype(F32).astype(BF16)
-    for k in range(3):
-        part = w.astype(BF16)
-        wmat[k] = lax.dot_general(eye, part, (((1,), (1,)), ((), ())),
-                                  preferred_element_type=F32).astype(BF16)
-        w = w - part.astype(F32)
+    @pl.loop(0, chunks // unroll)
+    def _(g):
+        products(nt - 1, g, activate)
+
+    @pl.loop(0, nt)
+    def _(src):
+        for k, (a, d) in enumerate(PIECES):
+            view = packed.at[src, pl.ds(0, dp - 1), pl.ds(a, d)]
+            pltpu.make_async_copy(view, view, d_send.at[src, k]).wait()
+
+    def gating():
+        @pl.loop(1, nt)
+        def _(i):
+            src = order(i)
+            pltpu.make_async_copy(lg_in.at[src], lg_in.at[src], lg_recv.at[src]).wait()
+
+        logits = jnp.sum(lg_in[...], axis=0)[:, 0:toks]
+        which = lax.broadcasted_iota(jnp.int32, logits.shape, 0)
+        chosen = [jnp.sum(jnp.where(which == idsv[k:k + 1, :], logits, 0.0), axis=0, keepdims=True)
+                  for k in range(2)]
+        first = jax.nn.sigmoid(chosen[0] - chosen[1])
+        w = hits[0] * first + hits[1] * (1.0 - first)
+        eye = (lax.broadcasted_iota(jnp.int32, (toks, toks), 0)
+               == lax.broadcasted_iota(jnp.int32, (toks, toks), 1)).astype(F32).astype(BF16)
+        for k in range(3):
+            part = w.astype(BF16)
+            wmat[k] = lax.dot_general(eye, part, (((1,), (1,)), ((), ())),
+                                      preferred_element_type=F32).astype(BF16)
+            w = w - part.astype(F32)
 
     @pl.loop(0, steps + LAG)
     def _(s):
@@ -226,18 +268,24 @@
                 term = sum(jnp.dot(hidden[:, b * kb:(b + 1) * kb],
                                    wbuf[slot, h, 0:kb, b * cb:(b + 1) * cb],
                                    preferred_element_type=F32) for b in range(kbs))
-                ret_out[s, :, :, pl.ds(h * cb, cb)] = term.astype(BF16).reshape(dp, PAD, cb)
+                packed[s // sub, :, :, pl.ds(pl.multiple_of((s % sub) * 2 * cb + h * cb, cb), cb)] = (
+                    term.astype(BF16).reshape(dp, PAD, cb))
             load(u + slots, lambda d: d.start())
-            ret_in[s, me] = ret_out[s, me]
+            cols = pl.ds(pl.multiple_of((s % sub) * 2 * cb, 2 * cb), 2 * cb)
+            ret_in[s, me] = packed[s // sub, me, :, cols]
 
             @pl.loop(1, dp)
             def _(i):
                 p = lax.rem(me + i, dp)
                 for k, (a, b) in enumerate(PIECES):
                     pltpu.make_async_remote_copy(
-                        ret_out.at[s, p, pl.ds(a, b)], ret_in.at[s, me, pl.ds(a, b)],
+                        packed.at[s // sub, p, pl.ds(a, b), cols], ret_in.at[s, me, pl.ds(a, b)],
                         r_send.at[s, k], r_recv.at[s, k],
                         device_id={"dp": p}, device_id_type=mesh).start()
+
+        @pl.when(s == LAG)
+        def _():
+            gating()
 
         @pl.when(s >= LAG)
         def _():
@@ -274,21 +322,27 @@
     for j in range(sub):
         out_ref[:, j * 2 * cb:(j + 1) * 2 * cb] = own[j].astype(BF16)
 
+    for h in range(2):
+        for k, (there, beside) in enumerate(sides):
+            @pl.when(there)
+            def _():
+                pltpu.make_async_copy(piece(tokv, h), piece(tokv, h), own_send.at[2 * h + k]).wait()
+
+            @pl.loop(0, nt)
+            def _(src):
+                @pl.when(there & ((src > t) if k == 0 else (src < t)))
+                def _():
+                    block = piece(ztok.at[src], h)
+                    pltpu.make_async_copy(block, block, zt_send.at[src, h]).wait()
+
     @pl.loop(1, nt)
     def _(i):
-        pltpu.make_async_copy(tokv, tokv, zt_send.at[i]).wait()
         pltpu.make_async_copy(lg_out, lg_out, lg_send.at[i]).wait()
-
-    @pl.loop(0, nt)
-    def _(src):
-        for k, (a, d) in enumerate(PIECES):
-            view = packed.at[src, pl.ds(0, dp - 1), pl.ds(a, d)]
-            pltpu.make_async_copy(view, view, d_send.at[src, k]).wait()
 
     @pl.loop(0, steps)
     def _(s):
         for k, (a, d) in enumerate(PIECES):
-            view = ret_out.at[s, pl.ds(0, dp - 1), pl.ds(a, d)]
+            view = ret_in.at[s, pl.ds(0, dp - 1), pl.ds(a, d)]
             pltpu.make_async_copy(view, view, r_send.at[s, k]).wait()
 
     @pl.loop(0, steps - sub)
@@ -321,7 +375,6 @@
             pltpu.VMEM((2, width, ff), F32),
             pltpu.VMEM((width, ff), BF16),
             pltpu.VMEM((steps, dp, PAD, 2 * cb), BF16),
-            pltpu.VMEM((steps, dp, PAD, 2 * cb), BF16),
             pltpu.VMEM((nt, toks, share), BF16),
             pltpu.VMEM((steps, toks, 2 * cb), BF16),
             pltpu.VMEM((nt, sub, toks, 2 * cb), BF16),
@@ -335,13 +388,13 @@
             pltpu.VMEM((2, toks), jnp.int32),
             dma((3,)),
             dma((2 * (ff // min(ff, share)) * slots,)),
-            dma((nt,)), dma((nt,)), dma((nt,)), dma((nt,)),
+            dma((4,)), dma((nt, 2)), dma((nt, 2)), dma((nt,)), dma((nt,)),
             dma((nt, 2)), dma((nt, 2)), dma((steps, 2)), dma((steps, 2)),
             dma((steps,)), dma((steps,)),
         ],
         compiler_params=pltpu.CompilerParams(
-            collective_id=0, has_side_effects=True, vmem_limit_bytes=67043328),
-    )(tokens, router_weight.T, expert_ids.T, w_gate[0], w_up[0], w_down[0])
+            collective_id=0, has_side_effects=True, vmem_limit_bytes=55836672),
+    )(*[pltpu.with_memory_space_constraint(x, pltpu.HBM) for x in (tokens, router_weight.T, expert_ids.T)], w_gate[0], w_up[0], w_down[0])
 
 
 def solution(mesh):

time: 50.1 us -> 45.7 us (0.912)
  Pallas kernels: 48.5 us -> 44.9 us
  local copies, waits for them, and re-layouts: 1.54 us -> 0.64 us
    pallas_call x1, Pallas kernels: 48.5 us -> 44.9 us  [per_device(): pl.pallas_call(functools.partial(body, dp, nt, n, cb, slots), out_shape=j...]
    unnamed x1, local copies, waits for them, and re-layouts: 1.54 us -> 0.64 us
where the time goes in v2:
time: 45.7 us; the launch traced here: 45.6 us
  Pallas kernels  44.9 us (98%)
  local copies, waits for them, and re-layouts  0.64 us (1%)
    pallas_call x1, Pallas kernels, per_device(): pl.pallas_call(functools.partial(body, dp, nt, n, cb, slots), out_shape=j...  44.9 us

profile of v2, /device:TPU:0, one launch (start us, length us, event | category | flops | bytes accessed | tf_op | source)
XLA Modules:
  0.0 45.6 jit_solution(10151134704895120430)
XLA Ops:
  0.0 44.9 %shard_map.64 = bf16[32,1536]{1,0:T(8,128)(2,1)S(1)} custom-call(bf16[32,1536]{1,0:T(8,128)(2,1)} %tok_hbm.1, bf16[8,1536]{1,0:T(8,128)(2,1)} %bitcast.8, s32[2,32]{1,0:T(2,128)} %bitcast.9, bf16[6144,3072]{1,0:T(8,128)(2,1)} %bitcast.5, bf16[6144,3072]{1,0:T(8,128)(2,1)} %bitcast.6, bf16[3072,6144]{1,0:T(8,128)(2,1)} %bitcast.7), custom_call_target="tpu_custom_call" | custom-call | tf_op jit(solution)/shard_map/pallas_call | solution.py:366
  44.9 0.6 %copy.8 = bf16[32,1536]{1,0:T(8,128)(2,1)} copy(bf16[32,1536]{1,0:T(8,128)(2,1)S(1)} %shard_map.64) | data formatting | bytes 196608
